TPU v7x, 32 devices: a whole 2x2x4 slice. The times are simulated.
32 devices in a mesh: sky: 8 (over y, x, core), tm: 4 (over z).
Axes of the slice: x: 2, y: 2, z: 4, core: 2. Of those that a mesh axis runs over, the one named last changes fastest.
Arguments:
- obs_source: int32 [131072], P(('sky', 'tm')), may hold values from 0 to 1023
- obs_knot: int32 [131072], P(('sky', 'tm')), may hold values from 0 to 2047, as said below
- obs_count: int32 [32], P(('sky', 'tm')), may hold values from 256 to 4096, as said below
- src_design: float32 [5, 131072], P(None, ('sky', 'tm')), may hold values from -3 to 3
- att_design: float32 [4, 131072], P(None, ('sky', 'tm')), may hold values from -6 to 6
- obs_phase: float32 [131072], P(('sky', 'tm')), may hold values from 0 to 1
- obs_value: float32 [131072], P(('sky', 'tm')), may hold values from -6 to 6
- src_prior: float32 [5, 8192], P(None, 'sky'), may hold values from 1 to 16
Outputs:
- att_solution: float32 [4, 4, 2048], P(None, 'tm', 'sky')
- att_residual: float32 [4, 4, 2048], P(None, 'tm', 'sky')
- source_solution: float32 [5, 8192], P(None, 'sky')
Inputs may be any that keep to these rules, and one draw needn't show every extreme that they name: Block b holds the 4096 observation slots o with o // 4096 = b; with i = b // 4 its sources are the sources i * 1024 + obs_source. With j = b % 4 for the observation's block b, its four spline knots are j * 2048 + obs_knot and the next three. In every block, each range of 256 values r * 256 to r * 256 + 255 of obs_knot holds exactly 512 of the block's slots. `obs_count`: each count is 4096 divided by 1, 2, 4, 8 or 16; the live slots of a block are its first ones; some block is full.
All inputs are finite; a program needn't handle non-finite values.
Results may differ from a plain program's by a relative error of at most 0.0001.
Values sent between devices are 32-bit elements; how exact they have to be, the bound alone decides.
A program may use at most 64 MiB of HBM per device.

v0:
```python
import jax
import jax.numpy as jnp
from jax import lax
from jax.sharding import PartitionSpec as P

ITERS = 2
SRC_DEV = 1024
KN_DEV = 256
damping = 0.5
entry_pairs = [(row_at, col_at) for row_at in range(5) for col_at in range(row_at + 1)]


def shifted(value, axis, steps):
    count = lax.axis_size(axis)
    first, last = (max(0, -steps), min(count, count - steps))
    return lax.ppermute(value, axis, [(source, source + steps) for source in range(first, last)])


def spline_taps(phase):
    squared = phase * phase
    cubed = squared * phase
    rest = 1.0 - phase
    return (
        rest * rest * rest / 6.0,
        (3.0 * cubed - 6.0 * squared + 4.0) / 6.0,
        (-3.0 * cubed + 3.0 * squared + 3.0 * phase + 1.0) / 6.0,
        cubed / 6.0,
    )


def factorize(normal):
    factor = {}
    for row_at in range(5):
        for col_at in range(row_at + 1):
            running = normal[row_at, col_at]
            for inner_at in range(col_at):
                running = running - factor[row_at, inner_at] * factor[col_at, inner_at]
            if row_at == col_at:
                factor[row_at, row_at] = jnp.sqrt(running)
            else:
                factor[row_at, col_at] = running / factor[col_at, col_at]
    return factor


def chol_solve(factor, target):
    forward = []
    for row_at in range(5):
        running = target[row_at]
        for inner_at in range(row_at):
            running = running - factor[row_at, inner_at] * forward[inner_at]
        forward.append(running / factor[row_at, row_at])
    result = [None] * 5
    for row_at in reversed(range(5)):
        running = forward[row_at]
        for inner_at in range(row_at + 1, 5):
            running = running - factor[inner_at, row_at] * result[inner_at]
        result[row_at] = running / factor[row_at, row_at]
    return jnp.stack(result)


def source_total(source, rows, count):
    return jnp.zeros((rows.shape[0], count), jnp.float32).at[:, source].add(rows)


def knot_values(padded, knot, design, tap_weights):
    summed = jnp.zeros(knot.shape, jnp.float32)
    for tap_at in range(4):
        picked = jnp.take(padded, knot + tap_at, axis=1)
        summed = summed + tap_weights[tap_at] * jnp.sum(design * picked, axis=0)
    return summed


def knot_total(knot, design, tap_weights, weight_vec, extent):
    summed = jnp.zeros((design.shape[0], extent + 3), jnp.float32)
    for tap_at in range(4):
        summed = summed.at[:, knot + tap_at].add(design * (tap_weights[tap_at] * weight_vec))
    return summed


def eliminate(factor, source, design, values_obs, source_sums):
    solved = chol_solve(factor, [source_sums[row_at] for row_at in range(5)])
    fitted = jnp.sum(design * jnp.take(solved, source, axis=1), axis=0)
    return values_obs - fitted


def shards(
    obs_source, obs_knot, obs_count, src_design, att_design, obs_phase, obs_value, src_prior
):
    sky_count = lax.axis_size("sky")
    seg_knots = KN_DEV * sky_count
    slot_count = obs_source.shape[0]
    live_mask = (jnp.arange(slot_count, dtype=jnp.int32) < obs_count[0]).astype(jnp.float32)
    src_rows = src_design * live_mask
    att_rows = att_design * live_mask
    observed = obs_value * live_mask
    tap_weights = spline_taps(obs_phase)
    products = jnp.stack(
        [src_rows[row_at] * src_rows[col_at] for row_at, col_at in entry_pairs]
        + [src_rows[row_at] * observed for row_at in range(5)]
    )
    sums = lax.psum(source_total(obs_source, products, SRC_DEV), "tm")
    normal = {}
    for entry_at, pair in enumerate(entry_pairs):
        normal[pair] = sums[entry_at] + (src_prior[pair[0]] if pair[0] == pair[1] else 0.0)
    factor = factorize(normal)

    def source_part(values_obs):
        return lax.psum(source_total(obs_source, src_rows * values_obs, SRC_DEV), "tm")

    def along_knots(field):
        segment = lax.all_gather(field, "sky", axis=1, tiled=True)
        next_edge = shifted(segment[:, :3], "tm", -1)
        padded = jnp.concatenate([segment, next_edge], axis=1)
        return knot_values(padded, obs_knot, att_rows, tap_weights)

    def back_to_knots(cleaned):
        summed = knot_total(obs_knot, att_rows, tap_weights, cleaned, seg_knots)
        overflow = shifted(summed[:, seg_knots:], "tm", 1)
        partial_value = summed[:, :seg_knots].at[:, :3].add(overflow)
        return lax.psum_scatter(partial_value, "sky", scatter_dimension=1, tiled=True)

    def norm_sum(partial_value):
        return lax.psum(partial_value, ("sky", "tm"))

    cleaned = eliminate(factor, obs_source, src_rows, observed, sums[15:])
    residual = back_to_knots(cleaned)
    solution = jnp.zeros_like(residual)
    direction = residual
    norm_now = norm_sum(jnp.sum(residual * residual))
    for repeat in range(ITERS):
        image_obs = along_knots(direction)
        cleaned = eliminate(factor, obs_source, src_rows, image_obs, source_part(image_obs))
        mapped = back_to_knots(cleaned) + damping * direction
        alpha_step = norm_now / lax.psum(jnp.sum(direction * mapped), ("sky", "tm"))
        solution = solution + alpha_step * direction
        residual = residual - alpha_step * mapped
        norm_next = norm_sum(jnp.sum(residual * residual))
        direction = residual + norm_next / norm_now * direction
        norm_now = norm_next
    fitted = observed - along_knots(solution)
    source_solution = chol_solve(factor, [row for row in source_part(fitted)])
    return (solution[:, None, :], residual[:, None, :], source_solution)


def solution(mesh):
    placed = (
        P(("sky", "tm")),
        P(("sky", "tm")),
        P(("sky", "tm")),
        P(None, ("sky", "tm")),
        P(None, ("sky", "tm")),
        P(("sky", "tm")),
        P(("sky", "tm")),
        P(None, "sky"),
    )
    return jax.shard_map(
        shards,
        mesh=mesh,
        in_specs=placed,
        out_specs=(P(None, "tm", "sky"), P(None, "tm", "sky"), P(None, "sky")),
        check_vma=False,
    )
```

profile of v0, /device:TPU:0, one launch (start us, length us, event | category | flops | bytes accessed | tf_op | source)
XLA Modules:
  0.0 1068.1 jit_solution(9590675632088410657)
XLA Ops:
  11.7 22.5 %scatter_custom_fusion = f32[20,1024]{0,1:T(8,128)S(1)} fusion(s32[4096]{0:T(1024)S(1)} %get-tuple-element.173, f32[4096,20]{1,0:T(8,128)S(1)} %copy.271, f32[]{:T(128)} %constant.111.clone.1), kind=kCustom, calls=%fused_computation.113 | custom fusion | flops 81920 | bytes 81924 | tf_op jit(solution)/shard_map/scatter-add | solution.py:62
  37.1 35.3 %all-reduce.3.cloned.1.call-done = f32[20,1024]{1,0:T(8,128)} async-done(((f32[20,1024]{1,0:T(8,128)}), f32[20,1024]{1,0:T(8,128)}) %all-reduce.3.cloned.1.call-update) | async-done | bytes 81936 | tf_op jit(solution)/shard_map/psum | solution.py:101
  73.6 1.6 subtract_divide_fusion.15
  75.5 14.1 %gather_fusion = f32[4096,5]{1,0:T(8,128)} fusion(f32[5,1024]{0,1:T(8,128)S(1)} %copy.273, s32[4096]{0:T(1024)S(1)} %get-tuple-element.172), kind=kCustom, calls=%fused_computation.clone | custom fusion | bytes 180224 | tf_op jit(solution)/shard_map/jit(_take)/gather | solution.py:82
  89.6 2.2 copy.274
  92.0 25.3 %scatter_custom_fusion.1 = f32[4,2051]{0,1:T(8,128)S(1)} fusion(s32[4096]{0:T(1024)} %get-tuple-element.168, f32[4096]{0:T(1024)S(1)} %get-tuple-element.159, f32[]{:T(128)} %constant.111.clone.1, f32[4,4096]{0,1:T(8,128)S(1)} %copy.270, f32[4096]{0:T(1024)S(1)} %fusion.83), kind=kCustom, calls=%fused_computation.77 | custom fusion | flops 49152 | bytes 131632 | tf_op jit(solution)/shard_map/scatter-add | solution.py:76
  117.3 25.4 %scatter_custom_fusion.2 = f32[4,2051]{0,1:T(8,128)S(1)} fusion(f32[4,2051]{0,1:T(8,128)S(1)} %scatter_custom_fusion.1, s32[4096]{0:T(1024)} %get-tuple-element.166, f32[4096]{0:T(1024)S(1)} %get-tuple-element.158, f32[4,4096]{0,1:T(8,128)S(1)} %copy.270, f32[4096]{0:T(1024)S(1)} %fusion.83), kind=kCustom, calls=%fused_computation.75 | custom fusion | flops 49152 | bytes 2162736 | tf_op jit(solution)/shard_map/scatter-add | solution.py:76
  142.6 25.4 %scatter_custom_fusion.3 = f32[4,2051]{0,1:T(8,128)S(1)} fusion(f32[4,2051]{0,1:T(8,128)S(1)} %scatter_custom_fusion.2, s32[4096]{0:T(1024)} %get-tuple-element.167, f32[4096]{0:T(1024)S(1)} %get-tuple-element.157, f32[4,4096]{0,1:T(8,128)S(1)} %copy.270, f32[4096]{0:T(1024)S(1)} %fusion.83), kind=kCustom, calls=%fused_computation.73 | custom fusion | flops 49152 | bytes 2162736 | tf_op jit(solution)/shard_map/scatter-add | solution.py:76
  168.1 25.4 %scatter_custom_fusion.4 = f32[4,2051]{0,1:T(8,128)S(1)} fusion(f32[4,2051]{0,1:T(8,128)S(1)} %scatter_custom_fusion.3, s32[4096]{0:T(1024)S(1)} %get-tuple-element.171, f32[4096]{0:T(1024)S(1)} %get-tuple-element.106, f32[4,4096]{0,1:T(8,128)S(1)} %copy.270, f32[4096]{0:T(1024)S(1)} %fusion.83), kind=kCustom, calls=%fused_computation.71 | custom fusion | flops 49152 | bytes 2162736 | tf_op jit(solution)/shard_map/scatter-add | solution.py:76
  194.6 3.3 collective-permute-start
  197.9 1.3 collective-permute-done
  199.8 1.3 scatter-add.132
  201.3 36.5 %reduce-scatter.10.cloned.1.call-done = f32[256,4]{1,0:T(8,128)} async-done(((f32[2048,4]{1,0:T(8,128)}), f32[256,4]{1,0:T(8,128)}) %reduce-scatter.10.cloned.1.call-update) | async-done | bytes 4112
  237.9 10.9 %all_gather.9 = f32[4,2048]{0,1:T(8,128)S(1)} all-gather(f32[4,256]{0,1:T(8,128)} %bitcast.131), channel_id=1, replica_groups=mesh['sky'=8,'tm'=4] {'sky'}, dimensions={1}, use_global_device_ids=true | all-gather | bytes 36864 | tf_op jit(solution)/shard_map/all_gather | solution.py:111
  248.8 1.3 collective-permute-start.1
  250.1 4.2 collective-permute-done.1
  254.3 14.1 %gather_fusion.4 = f32[4096,4]{1,0:T(8,128)} fusion(f32[4,2051]{0,1:T(8,128)S(1)} %constant_dynamic-update-slice_fusion, s32[4096]{0:T(1024)S(1)} %get-tuple-element.164), kind=kCustom, calls=%fused_computation.6.clone | custom fusion | bytes 147456 | tf_op jit(solution)/shard_map/jit(_take)/gather | solution.py:68
  268.4 14.1 %gather_fusion.3 = f32[4096,4]{1,0:T(8,128)} fusion(f32[4,2051]{0,1:T(8,128)S(1)} %constant_dynamic-update-slice_fusion, s32[4096]{0:T(1024)S(1)} %get-tuple-element.169), kind=kCustom, calls=%fused_computation.5.clone | custom fusion | bytes 147456 | tf_op jit(solution)/shard_map/jit(_take)/gather | solution.py:68
  282.5 14.1 %gather_fusion.2 = f32[4096,4]{1,0:T(8,128)} fusion(f32[4,2051]{0,1:T(8,128)S(1)} %constant_dynamic-update-slice_fusion, s32[4096]{0:T(1024)S(1)} %get-tuple-element.170), kind=kCustom, calls=%fused_computation.4.clone | custom fusion | bytes 147456 | tf_op jit(solution)/shard_map/jit(_take)/gather | solution.py:68
  296.5 14.1 %gather_fusion.1 = f32[4096,4]{1,0:T(8,128)} fusion(f32[4,2051]{0,1:T(8,128)S(1)} %constant_dynamic-update-slice_fusion, s32[4096]{0:T(1024)S(1)} %get-tuple-element.165), kind=kCustom, calls=%fused_computation.1.clone | custom fusion | bytes 147456 | tf_op jit(solution)/shard_map/jit(_take)/gather | solution.py:68
  310.6 8.9 fusion.27
  319.7 2.0 copy.277
  321.7 22.8 %scatter_custom_fusion.5 = f32[5,1024]{0,1:T(8,128)S(1)} fusion(s32[4096]{0:T(1024)} %copy-done.35, f32[4096,5]{1,0:T(8,128)} %copy.277, f32[]{:T(128)} %constant.111.clone.1), kind=kCustom, calls=%fused_computation.111 | custom fusion | flops 20480 | bytes 20992 | tf_op jit(solution)/shard_map/scatter-add | solution.py:62
  344.6 17.2 %psum.58 = f32[5,1024]{1,0:T(8,128)S(1)} all-reduce(f32[5,1024]{1,0:T(8,128)S(1)} %copy.278), channel_id=1, replica_groups=mesh['sky'=8,'tm'=4] {'tm'}, use_global_device_ids=true, to_apply=%region_16.19 | all-reduce | flops 5120 | bytes 40960 | tf_op jit(solution)/shard_map/psum | solution.py:108
  363.1 14.1 %gather_fusion.5 = f32[4096,5]{1,0:T(8,128)} fusion(f32[5,1024]{0,1:T(8,128)S(1)} %copy.279, s32[4096]{0:T(1024)S(1)} %get-tuple-element.172), kind=kCustom, calls=%fused_computation.2.clone | custom fusion | bytes 180224 | tf_op jit(solution)/shard_map/jit(_take)/gather | solution.py:82
  377.2 2.2 copy.280
  379.6 25.3 %scatter_custom_fusion.6 = f32[4,2051]{0,1:T(8,128)S(1)} fusion(s32[4096]{0:T(1024)} %get-tuple-element.168, f32[4096]{0:T(1024)S(1)} %get-tuple-element.156, f32[]{:T(128)} %constant.111.clone.1, f32[4,4096]{0,1:T(8,128)S(1)} %copy.270, f32[4096]{0:T(1024)S(1)} %fusion.83), kind=kCustom, calls=%fused_computation.61 | custom fusion | flops 49152 | bytes 131632 | tf_op jit(solution)/shard_map/scatter-add | solution.py:76
  404.8 25.6 %scatter_custom_fusion.7 = f32[4,2051]{0,1:T(8,128)S(1)} fusion(f32[4,2051]{0,1:T(8,128)S(1)} %scatter_custom_fusion.6, s32[4096]{0:T(1024)} %get-tuple-element.166, f32[4096]{0:T(1024)S(1)} %get-tuple-element.155, f32[4,4096]{0,1:T(8,128)S(1)} %copy.270, f32[4096]{0:T(1024)S(1)} %fusion.83), kind=kCustom, calls=%fused_computation.59 | custom fusion | flops 49152 | bytes 2162736 | tf_op jit(solution)/shard_map/scatter-add | solution.py:76
  430.5 25.4 %scatter_custom_fusion.8 = f32[4,2051]{0,1:T(8,128)S(1)} fusion(f32[4,2051]{0,1:T(8,128)S(1)} %scatter_custom_fusion.7, s32[4096]{0:T(1024)} %get-tuple-element.167, f32[4096]{0:T(1024)S(1)} %get-tuple-element.154, f32[4,4096]{0,1:T(8,128)S(1)} %copy.270, f32[4096]{0:T(1024)S(1)} %fusion.83), kind=kCustom, calls=%fused_computation.57 | custom fusion | flops 49152 | bytes 2162736 | tf_op jit(solution)/shard_map/scatter-add | solution.py:76
  455.8 25.4 %scatter_custom_fusion.9 = f32[4,2051]{0,1:T(8,128)S(1)} fusion(f32[4,2051]{0,1:T(8,128)S(1)} %scatter_custom_fusion.8, s32[4096]{0:T(1024)} %copy-done.36, f32[4096]{0:T(1024)S(1)} %get-tuple-element.95, f32[4,4096]{0,1:T(8,128)S(1)} %copy.270, f32[4096]{0:T(1024)S(1)} %fusion.83), kind=kCustom, calls=%fused_computation.55 | custom fusion | flops 49152 | bytes 2162736 | tf_op jit(solution)/shard_map/scatter-add | solution.py:76
  486.1 1.4 scatter-add.138
  487.6 36.2 %reduce-scatter.12.cloned.1.call-done = f32[256,4]{1,0:T(8,128)} async-done(((f32[2048,4]{1,0:T(8,128)}), f32[256,4]{1,0:T(8,128)}) %reduce-scatter.12.cloned.1.call-update) | async-done | bytes 4112
  525.4 39.5 %all-reduce = (f32[]{:T(128)}, f32[]{:T(128)}) all-reduce(f32[]{:T(128)} %get-tuple-element.72, f32[]{:T(128)} %get-tuple-element.71), channel_id=1, replica_groups=mesh['sky'=8,'tm'=4] {'sky','tm'}, use_global_device_ids=true, to_apply=%region_10.12 | all-reduce | flops 2 | bytes 16 | tf_op jit(solution)/shard_map/psum | solution.py:123
  566.7 41.3 %psum.60 = f32[]{:T(128)} all-reduce(f32[]{:T(128)} %multiply_reduce_fusion.1), channel_id=1, replica_groups=mesh['sky'=8,'tm'=4] {'sky','tm'}, use_global_device_ids=true, to_apply=%region_26.29 | all-reduce | flops 1 | bytes 8 | tf_op jit(solution)/shard_map/psum | solution.py:123
  609.2 10.1 all_gather.10
  619.3 1.7 collective-permute-start.3
  621.0 3.8 collective-permute-done.3
  625.2 14.1 %gather_fusion.9 = f32[4096,4]{1,0:T(8,128)} fusion(f32[4,2051]{0,1:T(8,128)S(1)} %copy.282, s32[4096]{0:T(1024)S(1)} %get-tuple-element.164), kind=kCustom, calls=%fused_computation.10.clone | custom fusion | bytes 147456 | tf_op jit(solution)/shard_map/jit(_take)/gather | solution.py:68
  639.2 14.1 %gather_fusion.8 = f32[4096,4]{1,0:T(8,128)} fusion(f32[4,2051]{0,1:T(8,128)S(1)} %copy.282, s32[4096]{0:T(1024)S(1)} %get-tuple-element.169), kind=kCustom, calls=%fused_computation.9.clone | custom fusion | bytes 147456 | tf_op jit(solution)/shard_map/jit(_take)/gather | solution.py:68
  653.3 14.1 %gather_fusion.7 = f32[4096,4]{1,0:T(8,128)} fusion(f32[4,2051]{0,1:T(8,128)S(1)} %copy.282, s32[4096]{0:T(1024)S(1)} %get-tuple-element.170), kind=kCustom, calls=%fused_computation.8.clone | custom fusion | bytes 147456 | tf_op jit(solution)/shard_map/jit(_take)/gather | solution.py:68
  667.4 14.1 %gather_fusion.6 = f32[4096,4]{1,0:T(8,128)} fusion(f32[4,2051]{0,1:T(8,128)S(1)} %copy.282, s32[4096]{0:T(1024)S(1)} %get-tuple-element.165), kind=kCustom, calls=%fused_computation.7.clone | custom fusion | bytes 147456 | tf_op jit(solution)/shard_map/jit(_take)/gather | solution.py:68
  681.5 9.5 fusion.15
  691.1 2.0 copy.286
  693.1 22.8 %scatter_custom_fusion.10 = f32[5,1024]{0,1:T(8,128)S(1)} fusion(s32[4096]{0:T(1024)} %copy-done.35, f32[4096,5]{1,0:T(8,128)} %copy.286, f32[]{:T(128)} %constant.111.clone.1), kind=kCustom, calls=%fused_computation.109 | custom fusion | flops 20480 | bytes 20992 | tf_op jit(solution)/shard_map/scatter-add | solution.py:62
  716.1 16.2 %psum.61 = f32[5,1024]{1,0:T(8,128)S(1)} all-reduce(f32[5,1024]{1,0:T(8,128)S(1)} %copy.287), channel_id=1, replica_groups=mesh['sky'=8,'tm'=4] {'tm'}, use_global_device_ids=true, to_apply=%region_32.35 | all-reduce | flops 5120 | bytes 40960 | tf_op jit(solution)/shard_map/psum | solution.py:108
  733.6 14.1 %gather_fusion.10 = f32[4096,5]{1,0:T(8,128)} fusion(f32[5,1024]{0,1:T(8,128)S(1)} %copy.288, s32[4096]{0:T(1024)S(1)} %get-tuple-element.172), kind=kCustom, calls=%fused_computation.3.clone | custom fusion | bytes 180224 | tf_op jit(solution)/shard_map/jit(_take)/gather | solution.py:82
  747.7 2.2 copy.289
  750.0 25.3 %scatter_custom_fusion.11 = f32[4,2051]{0,1:T(8,128)S(1)} fusion(s32[4096]{0:T(1024)} %get-tuple-element.168, f32[4096]{0:T(1024)S(1)} %get-tuple-element.153, f32[]{:T(128)} %constant.111.clone.1, f32[4,4096]{0,1:T(8,128)S(1)} %copy.270, f32[4096]{0:T(1024)S(1)} %fusion.83), kind=kCustom, calls=%fused_computation.45 | custom fusion | flops 49152 | bytes 131632 | tf_op jit(solution)/shard_map/scatter-add | solution.py:76
  775.3 25.4 %scatter_custom_fusion.12 = f32[4,2051]{0,1:T(8,128)S(1)} fusion(f32[4,2051]{0,1:T(8,128)S(1)} %scatter_custom_fusion.11, s32[4096]{0:T(1024)} %get-tuple-element.166, f32[4096]{0:T(1024)S(1)} %get-tuple-element.152, f32[4,4096]{0,1:T(8,128)S(1)} %copy.270, f32[4096]{0:T(1024)S(1)} %fusion.83), kind=kCustom, calls=%fused_computation.43 | custom fusion | flops 49152 | bytes 2162736 | tf_op jit(solution)/shard_map/scatter-add | solution.py:76
  800.7 25.4 %scatter_custom_fusion.13 = f32[4,2051]{0,1:T(8,128)S(1)} fusion(f32[4,2051]{0,1:T(8,128)S(1)} %scatter_custom_fusion.12, s32[4096]{0:T(1024)} %get-tuple-element.167, f32[4096]{0:T(1024)S(1)} %get-tuple-element.151, f32[4,4096]{0,1:T(8,128)S(1)} %copy.270, f32[4096]{0:T(1024)S(1)} %fusion.83), kind=kCustom, calls=%fused_computation.41 | custom fusion | flops 49152 | bytes 2162736 | tf_op jit(solution)/shard_map/scatter-add | solution.py:76
  826.1 25.6 %scatter_custom_fusion.14 = f32[4,2051]{0,1:T(8,128)S(1)} fusion(f32[4,2051]{0,1:T(8,128)S(1)} %scatter_custom_fusion.13, s32[4096]{0:T(1024)} %copy-done.36, f32[4096]{0:T(1024)S(1)} %get-tuple-element.84, f32[4,4096]{0,1:T(8,128)S(1)} %copy.270, f32[4096]{0:T(1024)S(1)} %fusion.83), kind=kCustom, calls=%fused_computation.39 | custom fusion | flops 49152 | bytes 2162736 | tf_op jit(solution)/shard_map/scatter-add | solution.py:76
  852.7 1.5 collective-permute-start.4
  856.1 1.3 scatter-add.144
  857.5 36.8 %reduce-scatter.14.cloned.1.call-done = f32[256,4]{1,0:T(8,128)} async-done(((f32[2048,4]{1,0:T(8,128)}), f32[256,4]{1,0:T(8,128)}) %reduce-scatter.14.cloned.1.call-update) | async-done | bytes 4112
  896.0 39.4 %psum.62 = f32[]{:T(128)} all-reduce(f32[]{:T(128)} %multiply_reduce_fusion), channel_id=1, replica_groups=mesh['sky'=8,'tm'=4] {'sky','tm'}, use_global_device_ids=true, to_apply=%region_40.43 | all-reduce | flops 1 | bytes 8 | tf_op jit(solution)/shard_map/psum | solution.py:134
  937.3 10.1 all_gather.11
  949.2 4.2 collective-permute-done.5
  953.8 14.1 %gather_fusion.14 = f32[4096,4]{1,0:T(8,128)} fusion(f32[4,2051]{0,1:T(8,128)S(1)} %copy.291, s32[4096]{0:T(1024)S(1)} %get-tuple-element.164), kind=kCustom, calls=%fused_computation.14.clone | custom fusion | bytes 147456 | tf_op jit(solution)/shard_map/jit(_take)/gather | solution.py:68
  967.9 14.1 %gather_fusion.13 = f32[4096,4]{1,0:T(8,128)} fusion(f32[4,2051]{0,1:T(8,128)S(1)} %copy.291, s32[4096]{0:T(1024)S(1)} %get-tuple-element.169), kind=kCustom, calls=%fused_computation.13.clone | custom fusion | bytes 147456 | tf_op jit(solution)/shard_map/jit(_take)/gather | solution.py:68
  982.0 14.1 %gather_fusion.12 = f32[4096,4]{1,0:T(8,128)} fusion(f32[4,2051]{0,1:T(8,128)S(1)} %copy.291, s32[4096]{0:T(1024)S(1)} %get-tuple-element.170), kind=kCustom, calls=%fused_computation.12.clone | custom fusion | bytes 147456 | tf_op jit(solution)/shard_map/jit(_take)/gather | solution.py:68
  996.0 14.1 %gather_fusion.11 = f32[4096,4]{1,0:T(8,128)} fusion(f32[4,2051]{0,1:T(8,128)S(1)} %copy.291, s32[4096]{0:T(1024)S(1)} %get-tuple-element.165), kind=kCustom, calls=%fused_computation.11.clone | custom fusion | bytes 147456 | tf_op jit(solution)/shard_map/jit(_take)/gather | solution.py:68
  1010.2 8.9 fusion.3
  1019.8 22.6 %scatter_custom_fusion.15 = f32[5,1024]{0,1:T(8,128)S(1)} fusion(s32[4096]{0:T(1024)} %copy-done.35, f32[4096,5]{1,0:T(8,128)S(1)} %copy.295, f32[]{:T(128)} %constant.111.clone.1), kind=kCustom, calls=%fused_computation.107 | custom fusion | flops 20480 | bytes 20992 | tf_op jit(solution)/shard_map/scatter-add | solution.py:62
  1042.6 17.2 %psum.63 = f32[5,1024]{1,0:T(8,128)S(1)} all-reduce(f32[5,1024]{1,0:T(8,128)S(1)} %copy.296), channel_id=1, replica_groups=mesh['sky'=8,'tm'=4] {'tm'}, use_global_device_ids=true, to_apply=%region_46.49 | all-reduce | flops 5120 | bytes 40960 | tf_op jit(solution)/shard_map/psum | solution.py:108
  (161 shorter events, 30.7 us)
Async XLA Ops:
  7.2 65.2 %all-reduce.3.cloned.1.call-start = ((), (), s32[]{:S(2)}) async-start(), calls=%async_computation.3 | async-start | bytes 196608 | tf_op jit(solution)/shard_map/psum | solution.py:101
  9.8 25.2 %copy-start.35 = (s32[4096]{0:T(1024)}, s32[4096]{0:T(1024)S(1)}, u32[]{:S(2)}) copy-start(s32[4096]{0:T(1024)S(1)} %get-tuple-element.173) | copy-start | bytes 49156
  10.5 24.6 %copy-start.25 = (s32[4096]{0:T(1024)S(1)}, s32[4096]{0:T(1024)}, u32[]{:S(2)}) copy-start(s32[4096]{0:T(1024)} %param.19) | copy-start | bytes 49156
  11.0 24.7 %copy-start.24 = (s32[4096]{0:T(1024)S(1)}, s32[4096]{0:T(1024)}, u32[]{:S(2)}) copy-start(s32[4096]{0:T(1024)} %param.18) | copy-start | bytes 49156
  11.0 24.7 %copy-start.23 = (f32[4,4096]{1,0:T(4,128)S(1)}, f32[4,4096]{1,0:T(4,128)}, u32[]{:S(2)}) copy-start(f32[4,4096]{1,0:T(4,128)} %param.22) | copy-start | bytes 196612
  11.7 60.7 %copy-start.34 = (f32[5,1024]{1,0:T(8,128)S(1)}, f32[5,1024]{1,0:T(8,128)}, u32[]{:S(2)}) copy-start(f32[5,1024]{1,0:T(8,128)} %param.25) | copy-start | bytes 61444
  35.0 202.8 %reduce-scatter.10.cloned.1.call-start = ((), (), s32[]{:S(2)}) async-start(), calls=%async_computation.4 | async-start | bytes 1179648
  35.7 132.3 %copy-start.36 = (s32[4096]{0:T(1024)}, s32[4096]{0:T(1024)S(1)}, u32[]{:S(2)}) copy-start(s32[4096]{0:T(1024)S(1)} %get-tuple-element.171) | copy-start | bytes 49156
  35.7 343.7 %copy-start.21 = (pred[4096]{0:T(1024)(128)(4,1)}, pred[4096]{0:T(1024)(128)(4,1)S(1)}, u32[]{:S(2)}) copy-start(pred[4096]{0:T(1024)(128)(4,1)S(1)} %compare_and_fusion.4) | copy-start | bytes 12292
  73.6 288.4 %copy-start.3 = (f32[1,1024]{1,0:T(1,128)}, f32[1,1024]{1,0:T(1,128)S(1)}, u32[]{:S(2)}) copy-start(f32[1,1024]{1,0:T(1,128)S(1)} %get-tuple-element.128) | copy-start | bytes 12292
  73.6 288.4 %copy-start.5 = (f32[1,1024]{1,0:T(1,128)}, f32[1,1024]{1,0:T(1,128)S(1)}, u32[]{:S(2)}) copy-start(f32[1,1024]{1,0:T(1,128)S(1)} %get-tuple-element.129) | copy-start | bytes 12292
  73.6 288.4 %copy-start.7 = (f32[1,1024]{1,0:T(1,128)}, f32[1,1024]{1,0:T(1,128)S(1)}, u32[]{:S(2)}) copy-start(f32[1,1024]{1,0:T(1,128)S(1)} %get-tuple-element.130) | copy-start | bytes 12292
  73.6 18.2 %copy-start = (f32[5,4096]{1,0:T(8,128)S(1)}, f32[5,4096]{1,0:T(8,128)}, u32[]{:S(2)}) copy-start(f32[5,4096]{1,0:T(8,128)} %param.21) | copy-start | bytes 245764
  75.3 16.6 %copy-start.1 = (f32[4096]{0:T(1024)S(1)}, f32[4096]{0:T(1024)}, u32[]{:S(2)}) copy-start(f32[4096]{0:T(1024)} %param.23) | copy-start | bytes 49156
  75.3 16.6 %copy-start.9 = (f32[4096]{0:T(1024)S(1)}, f32[4096]{0:T(1024)}, u32[]{:S(2)}) copy-start(f32[4096]{0:T(1024)} %param.24) | copy-start | bytes 49156
  194.6 4.6 collective-permute-start
  201.2 322.6 %reduce-scatter.12.cloned.1.call-start = ((), (), s32[]{:S(2)}) async-start(), calls=%async_computation.5 | async-start | bytes 1179648
  201.3 109.3 %copy-start.13 = (pred[4096]{0:T(1024)(128)(4,1)}, pred[4096]{0:T(1024)(128)(4,1)S(1)}, u32[]{:S(2)}) copy-start(pred[4096]{0:T(1024)(128)(4,1)S(1)} %get-tuple-element.160) | copy-start | bytes 12292
  201.3 109.3 %copy-start.15 = (pred[4096]{0:T(1024)(128)(4,1)}, pred[4096]{0:T(1024)(128)(4,1)S(1)}, u32[]{:S(2)}) copy-start(pred[4096]{0:T(1024)(128)(4,1)S(1)} %get-tuple-element.161) | copy-start | bytes 12292
  201.3 109.3 %copy-start.17 = (pred[4096]{0:T(1024)(128)(4,1)}, pred[4096]{0:T(1024)(128)(4,1)S(1)}, u32[]{:S(2)}) copy-start(pred[4096]{0:T(1024)(128)(4,1)S(1)} %get-tuple-element.162) | copy-start | bytes 12292
  201.3 109.3 %copy-start.19 = (pred[4096]{0:T(1024)(128)(4,1)}, pred[4096]{0:T(1024)(128)(4,1)S(1)}, u32[]{:S(2)}) copy-start(pred[4096]{0:T(1024)(128)(4,1)S(1)} %get-tuple-element.163) | copy-start | bytes 12292
  248.8 5.5 collective-permute-start.1
  319.6 42.4 %copy-start.26 = (f32[1,1024]{1,0:T(1,128)S(1)}, f32[1,1024]{1,0:T(1,128)}, u32[]{:S(2)}) copy-start(f32[1,1024]{1,0:T(1,128)} %get-tuple-element.113) | copy-start | bytes 12292
  319.6 42.4 %copy-start.28 = (f32[1,1024]{1,0:T(1,128)S(1)}, f32[1,1024]{1,0:T(1,128)}, u32[]{:S(2)}) copy-start(f32[1,1024]{1,0:T(1,128)} %get-tuple-element.114) | copy-start | bytes 12292
  319.6 42.4 %copy-start.30 = (f32[1,1024]{1,0:T(1,128)S(1)}, f32[1,1024]{1,0:T(1,128)}, u32[]{:S(2)}) copy-start(f32[1,1024]{1,0:T(1,128)} %get-tuple-element.115) | copy-start | bytes 12292
  319.6 42.4 %copy-start.32 = (f32[1,1024]{1,0:T(1,128)S(1)}, f32[1,1024]{1,0:T(1,128)}, u32[]{:S(2)}) copy-start(f32[1,1024]{1,0:T(1,128)} %get-tuple-element.116) | copy-start | bytes 12292
  481.2 6.3 copy-start.2
  482.3 2.6 collective-permute-start.2
  487.5 406.9 %reduce-scatter.14.cloned.1.call-start = ((), (), s32[]{:S(2)}) async-start(), calls=%async_computation.6 | async-start | bytes 1179648
  487.6 137.1 %copy-start.11 = (f32[4,256]{1,0:T(4,128)}, f32[4,256]{1,0:T(4,128)S(1)}, u32[]{:S(2)}) copy-start(f32[4,256]{1,0:T(4,128)S(1)} %copy.300) | copy-start | bytes 12292
  619.3 5.5 collective-permute-start.3
  691.0 41.3 %copy-start.4 = (f32[1,1024]{1,0:T(1,128)S(1)}, f32[1,1024]{1,0:T(1,128)}, u32[]{:S(2)}) copy-start(f32[1,1024]{1,0:T(1,128)} %copy-done.3) | copy-start | bytes 12292
  691.0 41.3 %copy-start.6 = (f32[1,1024]{1,0:T(1,128)S(1)}, f32[1,1024]{1,0:T(1,128)}, u32[]{:S(2)}) copy-start(f32[1,1024]{1,0:T(1,128)} %copy-done.5) | copy-start | bytes 12292
  691.0 41.3 %copy-start.8 = (f32[1,1024]{1,0:T(1,128)S(1)}, f32[1,1024]{1,0:T(1,128)}, u32[]{:S(2)}) copy-start(f32[1,1024]{1,0:T(1,128)} %copy-done.7) | copy-start | bytes 12292
  691.0 41.4 %copy-start.27 = (f32[1,1024]{1,0:T(1,128)S(1)}, f32[1,1024]{1,0:T(1,128)}, u32[]{:S(2)}) copy-start(f32[1,1024]{1,0:T(1,128)} %get-tuple-element.113) | copy-start | bytes 12292
  691.0 41.4 %copy-start.29 = (f32[1,1024]{1,0:T(1,128)S(1)}, f32[1,1024]{1,0:T(1,128)}, u32[]{:S(2)}) copy-start(f32[1,1024]{1,0:T(1,128)} %get-tuple-element.114) | copy-start | bytes 12292
  691.0 41.4 %copy-start.31 = (f32[1,1024]{1,0:T(1,128)S(1)}, f32[1,1024]{1,0:T(1,128)}, u32[]{:S(2)}) copy-start(f32[1,1024]{1,0:T(1,128)} %get-tuple-element.115) | copy-start | bytes 12292
  691.0 41.4 %copy-start.33 = (f32[1,1024]{1,0:T(1,128)S(1)}, f32[1,1024]{1,0:T(1,128)}, u32[]{:S(2)}) copy-start(f32[1,1024]{1,0:T(1,128)} %get-tuple-element.116) | copy-start | bytes 12292
  732.4 17.5 %copy-start.22 = (pred[4096]{0:T(1024)(128)(4,1)S(1)}, pred[4096]{0:T(1024)(128)(4,1)}, u32[]{:S(2)}) copy-start(pred[4096]{0:T(1024)(128)(4,1)} %copy-done.21) | copy-start | bytes 12292
  851.6 85.0 %copy-start.12 = (f32[4,256]{1,0:T(4,128)S(1)}, f32[4,256]{1,0:T(4,128)}, u32[]{:S(2)}) copy-start(f32[4,256]{1,0:T(4,128)} %copy-done.11) | copy-start | bytes 12292
  852.7 2.8 collective-permute-start.4
  857.5 152.6 %copy-start.14 = (pred[4096]{0:T(1024)(128)(4,1)S(1)}, pred[4096]{0:T(1024)(128)(4,1)}, u32[]{:S(2)}) copy-start(pred[4096]{0:T(1024)(128)(4,1)} %copy-done.13) | copy-start | bytes 12292
  857.5 152.6 %copy-start.16 = (pred[4096]{0:T(1024)(128)(4,1)S(1)}, pred[4096]{0:T(1024)(128)(4,1)}, u32[]{:S(2)}) copy-start(pred[4096]{0:T(1024)(128)(4,1)} %copy-done.15) | copy-start | bytes 12292
  857.5 152.6 %copy-start.18 = (pred[4096]{0:T(1024)(128)(4,1)S(1)}, pred[4096]{0:T(1024)(128)(4,1)}, u32[]{:S(2)}) copy-start(pred[4096]{0:T(1024)(128)(4,1)} %copy-done.17) | copy-start | bytes 12292
  857.5 152.6 %copy-start.20 = (pred[4096]{0:T(1024)(128)(4,1)S(1)}, pred[4096]{0:T(1024)(128)(4,1)}, u32[]{:S(2)}) copy-start(pred[4096]{0:T(1024)(128)(4,1)} %copy-done.19) | copy-start | bytes 12292
  948.0 5.5 collective-permute-start.5
  1010.1 9.0 copy-start.10
Sparse Core Ops, SparseCore 0:
  35.1 37.1 all-reduce.2
  201.3 36.4 reduce-scatter.9
  487.6 36.1 reduce-scatter.11
  857.6 36.7 reduce-scatter.13
where the time goes:
time: 1080 us; the launch traced here: 1070 us
  other arithmetic  437 us (40%)
  local copies, waits for them, and re-layouts  238 us (22%)
  blocking collectives  202 us (19%)
  waiting for transfers between devices  161 us (15%)
  between operations  19.3 us (2%)
    scatter-add x12, other arithmetic, knot_total(): summed.at[:, knot + tap_at].add(design * (tap_weights[tap_at] * weight_vec))  305 us
    gather x12, local copies, waits for them, and re-layouts, knot_values(): picked = jnp.take(padded, knot + tap_at, axis=1)  169 us
    unnamed x7, waiting for transfers between devices  110 us
    scatter-add x4, other arithmetic, source_total(): jnp.zeros((rows.shape[0], count), jnp.float32).at[:, source].add(rows)  90.6 us
    psum x2, blocking collectives, norm_sum(): return lax.psum(partial_value, ('sky', 'tm'))  80.7 us
    psum x3, blocking collectives, source_part(): lax.psum(source_total(obs_source, src_rows * values_obs, SRC_DEV), 'tm')  50.7 us
    gather x6, local copies, waits for them, and re-layouts, eliminate(): fitted = jnp.sum(design * jnp.take(solved, source, axis=1), axis=0)  48.9 us
    psum x1, blocking collectives, shards(): alpha_step = norm_now / lax.psum(jnp.sum(direction * mapped), ('sky', 'tm'))  39.4 us
  transfers between devices with their start and end apart: 10, of which 10 were waited for; matrix products, arithmetic and copies ran while one was open for 0% of the time, Pallas kernels for 0%

commit v1 on v0

--- a/solution.py
+++ b/solution.py
@@ -1,3 +1,4 @@
+import functools
 import jax
 import jax.numpy as jnp
 from jax import lax
@@ -8,6 +9,14 @@
 KN_DEV = 256
 damping = 0.5
 entry_pairs = [(row_at, col_at) for row_at in range(5) for col_at in range(row_at + 1)]
+
+
+def map_body(obj, which_axis):
+    p_next = lax.all_gather(obj, which_axis).sum(axis=0)
+    return p_next
+
+
+fix_bars = functools.partial(map_body, which_axis=("sky", "tm"))
 
 
 def shifted(value, axis, steps):
@@ -120,7 +129,7 @@
         return lax.psum_scatter(partial_value, "sky", scatter_dimension=1, tiled=True)
 
     def norm_sum(partial_value):
-        return lax.psum(partial_value, ("sky", "tm"))
+        return fix_bars(partial_value)
 
     cleaned = eliminate(factor, obs_source, src_rows, observed, sums[15:])
     residual = back_to_knots(cleaned)

time: 1080 us -> 1080 us (level)
    psum x2 -> x0, blocking collectives: 80.7 us -> none  [norm_sum(): return lax.psum(partial_value, ('sky', 'tm'))]
    unnamed x0 -> x2, blocking collectives: none -> 80.5 us
where the time goes in v1:
time: 1080 us; the launch traced here: 1070 us
  other arithmetic  438 us (41%)
  local copies, waits for them, and re-layouts  240 us (22%)
  blocking collectives  201 us (19%)
  waiting for transfers between devices  161 us (15%)
  between operations  19.4 us (2%)
    scatter-add x12, other arithmetic, knot_total(): summed.at[:, knot + tap_at].add(design * (tap_weights[tap_at] * weight_vec))  305 us
    gather x12, local copies, waits for them, and re-layouts, knot_values(): picked = jnp.take(padded, knot + tap_at, axis=1)  169 us
    unnamed x7, waiting for transfers between devices  110 us
    scatter-add x4, other arithmetic, source_total(): jnp.zeros((rows.shape[0], count), jnp.float32).at[:, source].add(rows)  90.6 us
    unnamed x2, blocking collectives  80.5 us
    psum x3, blocking collectives, source_part(): lax.psum(source_total(obs_source, src_rows * values_obs, SRC_DEV), 'tm')  50.6 us
    gather x6, local copies, waits for them, and re-layouts, eliminate(): fitted = jnp.sum(design * jnp.take(solved, source, axis=1), axis=0)  48.9 us
    psum x1, blocking collectives, shards(): alpha_step = norm_now / lax.psum(jnp.sum(direction * mapped), ('sky', 'tm'))  39.5 us
  transfers between devices with their start and end apart: 10, of which 10 were waited for; matrix products, arithmetic and copies ran while one was open for 0% of the time, Pallas kernels for 0%

profile of v1, /device:TPU:0, one launch (start us, length us, event | category | flops | bytes accessed | tf_op | source)
XLA Modules:
  0.0 1070.4 jit_solution(15198423477817513377)
XLA Ops:
  11.7 22.5 %scatter_custom_fusion = f32[20,1024]{0,1:T(8,128)S(1)} fusion(s32[4096]{0:T(1024)S(1)} %get-tuple-element.173, f32[4096,20]{1,0:T(8,128)S(1)} %copy.271, f32[]{:T(128)} %constant.111.clone.1), kind=kCustom, calls=%fused_computation.113 | custom fusion | flops 81920 | bytes 81924 | tf_op jit(solution)/shard_map/scatter-add | solution.py:71
  37.1 35.3 %all-reduce.5.cloned.1.call-done = f32[20,1024]{1,0:T(8,128)} async-done(((f32[20,1024]{1,0:T(8,128)}), f32[20,1024]{1,0:T(8,128)}) %all-reduce.5.cloned.1.call-update) | async-done | bytes 81936 | tf_op jit(solution)/shard_map/psum | solution.py:110
  73.6 1.6 subtract_divide_fusion.15
  75.5 14.1 %gather_fusion = f32[4096,5]{1,0:T(8,128)} fusion(f32[5,1024]{0,1:T(8,128)S(1)} %copy.273, s32[4096]{0:T(1024)S(1)} %get-tuple-element.172), kind=kCustom, calls=%fused_computation.clone | custom fusion | bytes 180224 | tf_op jit(solution)/shard_map/jit(_take)/gather | solution.py:91
  89.6 2.2 copy.274
  92.0 25.3 %scatter_custom_fusion.1 = f32[4,2051]{0,1:T(8,128)S(1)} fusion(s32[4096]{0:T(1024)} %get-tuple-element.168, f32[4096]{0:T(1024)S(1)} %get-tuple-element.159, f32[]{:T(128)} %constant.111.clone.1, f32[4,4096]{0,1:T(8,128)S(1)} %copy.270, f32[4096]{0:T(1024)S(1)} %fusion.83), kind=kCustom, calls=%fused_computation.77 | custom fusion | flops 49152 | bytes 131632 | tf_op jit(solution)/shard_map/scatter-add | solution.py:85
  117.3 25.4 %scatter_custom_fusion.2 = f32[4,2051]{0,1:T(8,128)S(1)} fusion(f32[4,2051]{0,1:T(8,128)S(1)} %scatter_custom_fusion.1, s32[4096]{0:T(1024)} %get-tuple-element.166, f32[4096]{0:T(1024)S(1)} %get-tuple-element.158, f32[4,4096]{0,1:T(8,128)S(1)} %copy.270, f32[4096]{0:T(1024)S(1)} %fusion.83), kind=kCustom, calls=%fused_computation.75 | custom fusion | flops 49152 | bytes 2162736 | tf_op jit(solution)/shard_map/scatter-add | solution.py:85
  142.6 25.4 %scatter_custom_fusion.3 = f32[4,2051]{0,1:T(8,128)S(1)} fusion(f32[4,2051]{0,1:T(8,128)S(1)} %scatter_custom_fusion.2, s32[4096]{0:T(1024)} %get-tuple-element.167, f32[4096]{0:T(1024)S(1)} %get-tuple-element.157, f32[4,4096]{0,1:T(8,128)S(1)} %copy.270, f32[4096]{0:T(1024)S(1)} %fusion.83), kind=kCustom, calls=%fused_computation.73 | custom fusion | flops 49152 | bytes 2162736 | tf_op jit(solution)/shard_map/scatter-add | solution.py:85
  168.1 25.4 %scatter_custom_fusion.4 = f32[4,2051]{0,1:T(8,128)S(1)} fusion(f32[4,2051]{0,1:T(8,128)S(1)} %scatter_custom_fusion.3, s32[4096]{0:T(1024)S(1)} %get-tuple-element.171, f32[4096]{0:T(1024)S(1)} %get-tuple-element.106, f32[4,4096]{0,1:T(8,128)S(1)} %copy.270, f32[4096]{0:T(1024)S(1)} %fusion.83), kind=kCustom, calls=%fused_computation.71 | custom fusion | flops 49152 | bytes 2162736 | tf_op jit(solution)/shard_map/scatter-add | solution.py:85
  194.6 3.3 collective-permute-start
  197.9 1.3 collective-permute-done
  199.8 1.3 scatter-add.132
  201.3 36.5 %reduce-scatter.10.cloned.1.call-done = f32[256,4]{1,0:T(8,128)} async-done(((f32[2048,4]{1,0:T(8,128)}), f32[256,4]{1,0:T(8,128)}) %reduce-scatter.10.cloned.1.call-update) | async-done | bytes 4112
  237.8 10.9 %all_gather.23 = f32[4,2048]{0,1:T(8,128)S(1)} all-gather(f32[4,256]{0,1:T(8,128)} %bitcast.133), channel_id=1, replica_groups=mesh['sky'=8,'tm'=4] {'sky'}, dimensions={1}, use_global_device_ids=true | all-gather | bytes 36864 | tf_op jit(solution)/shard_map/all_gather | solution.py:120
  248.8 1.3 collective-permute-start.1
  250.1 4.2 collective-permute-done.1
  254.3 14.1 %gather_fusion.1 = f32[4096,4]{1,0:T(8,128)} fusion(f32[4,2051]{0,1:T(8,128)S(1)} %constant_dynamic-update-slice_fusion, s32[4096]{0:T(1024)S(1)} %get-tuple-element.165), kind=kCustom, calls=%fused_computation.1.clone | custom fusion | bytes 147456 | tf_op jit(solution)/shard_map/jit(_take)/gather | solution.py:77
  268.4 14.1 %gather_fusion.2 = f32[4096,4]{1,0:T(8,128)} fusion(f32[4,2051]{0,1:T(8,128)S(1)} %constant_dynamic-update-slice_fusion, s32[4096]{0:T(1024)S(1)} %get-tuple-element.170), kind=kCustom, calls=%fused_computation.4.clone | custom fusion | bytes 147456 | tf_op jit(solution)/shard_map/jit(_take)/gather | solution.py:77
  282.5 14.1 %gather_fusion.3 = f32[4096,4]{1,0:T(8,128)} fusion(f32[4,2051]{0,1:T(8,128)S(1)} %constant_dynamic-update-slice_fusion, s32[4096]{0:T(1024)S(1)} %get-tuple-element.169), kind=kCustom, calls=%fused_computation.5.clone | custom fusion | bytes 147456 | tf_op jit(solution)/shard_map/jit(_take)/gather | solution.py:77
  296.5 14.1 %gather_fusion.4 = f32[4096,4]{1,0:T(8,128)} fusion(f32[4,2051]{0,1:T(8,128)S(1)} %constant_dynamic-update-slice_fusion, s32[4096]{0:T(1024)S(1)} %get-tuple-element.164), kind=kCustom, calls=%fused_computation.6.clone | custom fusion | bytes 147456 | tf_op jit(solution)/shard_map/jit(_take)/gather | solution.py:77
  310.6 8.9 fusion.27
  319.7 2.0 copy.277
  321.7 22.8 %scatter_custom_fusion.5 = f32[5,1024]{0,1:T(8,128)S(1)} fusion(s32[4096]{0:T(1024)} %copy-done.35, f32[4096,5]{1,0:T(8,128)} %copy.277, f32[]{:T(128)} %constant.111.clone.1), kind=kCustom, calls=%fused_computation.111 | custom fusion | flops 20480 | bytes 20992 | tf_op jit(solution)/shard_map/scatter-add | solution.py:71
  344.6 17.2 %psum.43 = f32[5,1024]{1,0:T(8,128)S(1)} all-reduce(f32[5,1024]{1,0:T(8,128)S(1)} %copy.278), channel_id=1, replica_groups=mesh['sky'=8,'tm'=4] {'tm'}, use_global_device_ids=true, to_apply=%region_16.19 | all-reduce | flops 5120 | bytes 40960 | tf_op jit(solution)/shard_map/psum | solution.py:117
  363.1 14.1 %gather_fusion.5 = f32[4096,5]{1,0:T(8,128)} fusion(f32[5,1024]{0,1:T(8,128)S(1)} %copy.279, s32[4096]{0:T(1024)S(1)} %get-tuple-element.172), kind=kCustom, calls=%fused_computation.2.clone | custom fusion | bytes 180224 | tf_op jit(solution)/shard_map/jit(_take)/gather | solution.py:91
  377.2 2.2 copy.280
  379.6 25.3 %scatter_custom_fusion.6 = f32[4,2051]{0,1:T(8,128)S(1)} fusion(s32[4096]{0:T(1024)} %get-tuple-element.168, f32[4096]{0:T(1024)S(1)} %get-tuple-element.156, f32[]{:T(128)} %constant.111.clone.1, f32[4,4096]{0,1:T(8,128)S(1)} %copy.270, f32[4096]{0:T(1024)S(1)} %fusion.83), kind=kCustom, calls=%fused_computation.61 | custom fusion | flops 49152 | bytes 131632 | tf_op jit(solution)/shard_map/scatter-add | solution.py:85
  404.8 25.6 %scatter_custom_fusion.7 = f32[4,2051]{0,1:T(8,128)S(1)} fusion(f32[4,2051]{0,1:T(8,128)S(1)} %scatter_custom_fusion.6, s32[4096]{0:T(1024)} %get-tuple-element.166, f32[4096]{0:T(1024)S(1)} %get-tuple-element.155, f32[4,4096]{0,1:T(8,128)S(1)} %copy.270, f32[4096]{0:T(1024)S(1)} %fusion.83), kind=kCustom, calls=%fused_computation.59 | custom fusion | flops 49152 | bytes 2162736 | tf_op jit(solution)/shard_map/scatter-add | solution.py:85
  430.5 25.4 %scatter_custom_fusion.8 = f32[4,2051]{0,1:T(8,128)S(1)} fusion(f32[4,2051]{0,1:T(8,128)S(1)} %scatter_custom_fusion.7, s32[4096]{0:T(1024)} %get-tuple-element.167, f32[4096]{0:T(1024)S(1)} %get-tuple-element.154, f32[4,4096]{0,1:T(8,128)S(1)} %copy.270, f32[4096]{0:T(1024)S(1)} %fusion.83), kind=kCustom, calls=%fused_computation.57 | custom fusion | flops 49152 | bytes 2162736 | tf_op jit(solution)/shard_map/scatter-add | solution.py:85
  455.8 25.4 %scatter_custom_fusion.9 = f32[4,2051]{0,1:T(8,128)S(1)} fusion(f32[4,2051]{0,1:T(8,128)S(1)} %scatter_custom_fusion.8, s32[4096]{0:T(1024)} %copy-done.36, f32[4096]{0:T(1024)S(1)} %get-tuple-element.95, f32[4,4096]{0,1:T(8,128)S(1)} %copy.270, f32[4096]{0:T(1024)S(1)} %fusion.83), kind=kCustom, calls=%fused_computation.55 | custom fusion | flops 49152 | bytes 2162736 | tf_op jit(solution)/shard_map/scatter-add | solution.py:85
  486.1 1.4 scatter-add.138
  487.6 36.1 %reduce-scatter.12.cloned.1.call-done = f32[256,4]{1,0:T(8,128)} async-done(((f32[2048,4]{1,0:T(8,128)}), f32[256,4]{1,0:T(8,128)}) %reduce-scatter.12.cloned.1.call-update) | async-done | bytes 4112
  526.1 39.5 %all-reduce.2 = (f32[32]{0:T(128)S(1)}, f32[]{:T(128)}) all-reduce(f32[32]{0:T(128)S(1)} %dynamic-update-slice.9, f32[]{:T(128)} %get-tuple-element.71), channel_id=1, replica_groups=mesh['sky'=8,'tm'=4] {'sky','tm'}, use_global_device_ids=true, to_apply=%add | all-reduce | flops 33 | bytes 264
  568.7 41.1 %all-reduce.1 = f32[32]{0:T(128)S(1)} all-reduce(f32[32]{0:T(128)S(1)} %dynamic-update-slice.10), channel_id=1, replica_groups=mesh['sky'=8,'tm'=4] {'sky','tm'}, use_global_device_ids=true, to_apply=%add.1 | all-reduce | flops 32 | bytes 256
  611.7 9.9 all_gather.26
  621.6 1.7 collective-permute-start.3
  623.3 3.8 collective-permute-done.3
  627.4 14.1 %gather_fusion.6 = f32[4096,4]{1,0:T(8,128)} fusion(f32[4,2051]{0,1:T(8,128)S(1)} %copy.282, s32[4096]{0:T(1024)S(1)} %get-tuple-element.165), kind=kCustom, calls=%fused_computation.7.clone | custom fusion | bytes 147456 | tf_op jit(solution)/shard_map/jit(_take)/gather | solution.py:77
  641.5 14.1 %gather_fusion.7 = f32[4096,4]{1,0:T(8,128)} fusion(f32[4,2051]{0,1:T(8,128)S(1)} %copy.282, s32[4096]{0:T(1024)S(1)} %get-tuple-element.170), kind=kCustom, calls=%fused_computation.8.clone | custom fusion | bytes 147456 | tf_op jit(solution)/shard_map/jit(_take)/gather | solution.py:77
  655.6 14.1 %gather_fusion.8 = f32[4096,4]{1,0:T(8,128)} fusion(f32[4,2051]{0,1:T(8,128)S(1)} %copy.282, s32[4096]{0:T(1024)S(1)} %get-tuple-element.169), kind=kCustom, calls=%fused_computation.9.clone | custom fusion | bytes 147456 | tf_op jit(solution)/shard_map/jit(_take)/gather | solution.py:77
  669.7 14.1 %gather_fusion.9 = f32[4096,4]{1,0:T(8,128)} fusion(f32[4,2051]{0,1:T(8,128)S(1)} %copy.282, s32[4096]{0:T(1024)S(1)} %get-tuple-element.164), kind=kCustom, calls=%fused_computation.10.clone | custom fusion | bytes 147456 | tf_op jit(solution)/shard_map/jit(_take)/gather | solution.py:77
  683.7 9.5 fusion.15
  693.4 2.0 copy.286
  695.4 22.8 %scatter_custom_fusion.10 = f32[5,1024]{0,1:T(8,128)S(1)} fusion(s32[4096]{0:T(1024)} %copy-done.35, f32[4096,5]{1,0:T(8,128)} %copy.286, f32[]{:T(128)} %constant.111.clone.1), kind=kCustom, calls=%fused_computation.109 | custom fusion | flops 20480 | bytes 20992 | tf_op jit(solution)/shard_map/scatter-add | solution.py:71
  718.3 16.2 %psum.45 = f32[5,1024]{1,0:T(8,128)S(1)} all-reduce(f32[5,1024]{1,0:T(8,128)S(1)} %copy.287), channel_id=1, replica_groups=mesh['sky'=8,'tm'=4] {'tm'}, use_global_device_ids=true, to_apply=%region_32.35 | all-reduce | flops 5120 | bytes 40960 | tf_op jit(solution)/shard_map/psum | solution.py:117
  735.8 14.1 %gather_fusion.10 = f32[4096,5]{1,0:T(8,128)} fusion(f32[5,1024]{0,1:T(8,128)S(1)} %copy.288, s32[4096]{0:T(1024)S(1)} %get-tuple-element.172), kind=kCustom, calls=%fused_computation.3.clone | custom fusion | bytes 180224 | tf_op jit(solution)/shard_map/jit(_take)/gather | solution.py:91
  749.9 2.2 copy.289
  752.3 25.3 %scatter_custom_fusion.11 = f32[4,2051]{0,1:T(8,128)S(1)} fusion(s32[4096]{0:T(1024)} %get-tuple-element.168, f32[4096]{0:T(1024)S(1)} %get-tuple-element.153, f32[]{:T(128)} %constant.111.clone.1, f32[4,4096]{0,1:T(8,128)S(1)} %copy.270, f32[4096]{0:T(1024)S(1)} %fusion.83), kind=kCustom, calls=%fused_computation.45 | custom fusion | flops 49152 | bytes 131632 | tf_op jit(solution)/shard_map/scatter-add | solution.py:85
  777.5 25.4 %scatter_custom_fusion.12 = f32[4,2051]{0,1:T(8,128)S(1)} fusion(f32[4,2051]{0,1:T(8,128)S(1)} %scatter_custom_fusion.11, s32[4096]{0:T(1024)} %get-tuple-element.166, f32[4096]{0:T(1024)S(1)} %get-tuple-element.152, f32[4,4096]{0,1:T(8,128)S(1)} %copy.270, f32[4096]{0:T(1024)S(1)} %fusion.83), kind=kCustom, calls=%fused_computation.43 | custom fusion | flops 49152 | bytes 2162736 | tf_op jit(solution)/shard_map/scatter-add | solution.py:85
  802.9 25.4 %scatter_custom_fusion.13 = f32[4,2051]{0,1:T(8,128)S(1)} fusion(f32[4,2051]{0,1:T(8,128)S(1)} %scatter_custom_fusion.12, s32[4096]{0:T(1024)} %get-tuple-element.167, f32[4096]{0:T(1024)S(1)} %get-tuple-element.151, f32[4,4096]{0,1:T(8,128)S(1)} %copy.270, f32[4096]{0:T(1024)S(1)} %fusion.83), kind=kCustom, calls=%fused_computation.41 | custom fusion | flops 49152 | bytes 2162736 | tf_op jit(solution)/shard_map/scatter-add | solution.py:85
  828.3 25.6 %scatter_custom_fusion.14 = f32[4,2051]{0,1:T(8,128)S(1)} fusion(f32[4,2051]{0,1:T(8,128)S(1)} %scatter_custom_fusion.13, s32[4096]{0:T(1024)} %copy-done.36, f32[4096]{0:T(1024)S(1)} %get-tuple-element.84, f32[4,4096]{0,1:T(8,128)S(1)} %copy.270, f32[4096]{0:T(1024)S(1)} %fusion.83), kind=kCustom, calls=%fused_computation.39 | custom fusion | flops 49152 | bytes 2162736 | tf_op jit(solution)/shard_map/scatter-add | solution.py:85
  855.0 1.5 collective-permute-start.4
  858.4 1.3 scatter-add.144
  859.8 36.9 %reduce-scatter.14.cloned.1.call-done = f32[256,4]{1,0:T(8,128)} async-done(((f32[2048,4]{1,0:T(8,128)}), f32[256,4]{1,0:T(8,128)}) %reduce-scatter.14.cloned.1.call-update) | async-done | bytes 4112
  898.2 39.5 %psum.46 = f32[]{:T(128)} all-reduce(f32[]{:T(128)} %multiply_reduce_fusion), channel_id=1, replica_groups=mesh['sky'=8,'tm'=4] {'sky','tm'}, use_global_device_ids=true, to_apply=%region_40.43 | all-reduce | flops 1 | bytes 8 | tf_op jit(solution)/shard_map/psum | solution.py:143
  939.1 10.1 all_gather.27
  951.6 4.2 collective-permute-done.5
  956.2 14.1 %gather_fusion.11 = f32[4096,4]{1,0:T(8,128)} fusion(f32[4,2051]{0,1:T(8,128)S(1)} %copy.291, s32[4096]{0:T(1024)S(1)} %get-tuple-element.165), kind=kCustom, calls=%fused_computation.11.clone | custom fusion | bytes 147456 | tf_op jit(solution)/shard_map/jit(_take)/gather | solution.py:77
  970.3 14.1 %gather_fusion.12 = f32[4096,4]{1,0:T(8,128)} fusion(f32[4,2051]{0,1:T(8,128)S(1)} %copy.291, s32[4096]{0:T(1024)S(1)} %get-tuple-element.170), kind=kCustom, calls=%fused_computation.12.clone | custom fusion | bytes 147456 | tf_op jit(solution)/shard_map/jit(_take)/gather | solution.py:77
  984.3 14.1 %gather_fusion.13 = f32[4096,4]{1,0:T(8,128)} fusion(f32[4,2051]{0,1:T(8,128)S(1)} %copy.291, s32[4096]{0:T(1024)S(1)} %get-tuple-element.169), kind=kCustom, calls=%fused_computation.13.clone | custom fusion | bytes 147456 | tf_op jit(solution)/shard_map/jit(_take)/gather | solution.py:77
  998.4 14.1 %gather_fusion.14 = f32[4096,4]{1,0:T(8,128)} fusion(f32[4,2051]{0,1:T(8,128)S(1)} %copy.291, s32[4096]{0:T(1024)S(1)} %get-tuple-element.164), kind=kCustom, calls=%fused_computation.14.clone | custom fusion | bytes 147456 | tf_op jit(solution)/shard_map/jit(_take)/gather | solution.py:77
  1012.5 8.9 fusion.3
  1022.2 22.6 %scatter_custom_fusion.15 = f32[5,1024]{0,1:T(8,128)S(1)} fusion(s32[4096]{0:T(1024)} %copy-done.35, f32[4096,5]{1,0:T(8,128)S(1)} %copy.295, f32[]{:T(128)} %constant.111.clone.1), kind=kCustom, calls=%fused_computation.107 | custom fusion | flops 20480 | bytes 20992 | tf_op jit(solution)/shard_map/scatter-add | solution.py:71
  1045.0 17.1 %psum.47 = f32[5,1024]{1,0:T(8,128)S(1)} all-reduce(f32[5,1024]{1,0:T(8,128)S(1)} %copy.296), channel_id=1, replica_groups=mesh['sky'=8,'tm'=4] {'tm'}, use_global_device_ids=true, to_apply=%region_46.49 | all-reduce | flops 5120 | bytes 40960 | tf_op jit(solution)/shard_map/psum | solution.py:117
  (167 shorter events, 33.4 us)
Async XLA Ops:
  7.2 65.2 %all-reduce.5.cloned.1.call-start = ((), (), s32[]{:S(2)}) async-start(), calls=%async_computation.3 | async-start | bytes 196608 | tf_op jit(solution)/shard_map/psum | solution.py:110
  9.8 25.2 %copy-start.35 = (s32[4096]{0:T(1024)}, s32[4096]{0:T(1024)S(1)}, u32[]{:S(2)}) copy-start(s32[4096]{0:T(1024)S(1)} %get-tuple-element.173) | copy-start | bytes 49156
  10.5 24.6 %copy-start.25 = (s32[4096]{0:T(1024)S(1)}, s32[4096]{0:T(1024)}, u32[]{:S(2)}) copy-start(s32[4096]{0:T(1024)} %param.19) | copy-start | bytes 49156
  11.0 24.7 %copy-start.24 = (s32[4096]{0:T(1024)S(1)}, s32[4096]{0:T(1024)}, u32[]{:S(2)}) copy-start(s32[4096]{0:T(1024)} %param.18) | copy-start | bytes 49156
  11.0 24.7 %copy-start.23 = (f32[4,4096]{1,0:T(4,128)S(1)}, f32[4,4096]{1,0:T(4,128)}, u32[]{:S(2)}) copy-start(f32[4,4096]{1,0:T(4,128)} %param.22) | copy-start | bytes 196612
  11.7 60.7 %copy-start.34 = (f32[5,1024]{1,0:T(8,128)S(1)}, f32[5,1024]{1,0:T(8,128)}, u32[]{:S(2)}) copy-start(f32[5,1024]{1,0:T(8,128)} %param.25) | copy-start | bytes 61444
  35.0 202.8 %reduce-scatter.10.cloned.1.call-start = ((), (), s32[]{:S(2)}) async-start(), calls=%async_computation.4 | async-start | bytes 1179648
  35.7 132.3 %copy-start.36 = (s32[4096]{0:T(1024)}, s32[4096]{0:T(1024)S(1)}, u32[]{:S(2)}) copy-start(s32[4096]{0:T(1024)S(1)} %get-tuple-element.171) | copy-start | bytes 49156
  35.7 343.7 %copy-start.21 = (pred[4096]{0:T(1024)(128)(4,1)}, pred[4096]{0:T(1024)(128)(4,1)S(1)}, u32[]{:S(2)}) copy-start(pred[4096]{0:T(1024)(128)(4,1)S(1)} %compare_and_fusion.4) | copy-start | bytes 12292
  73.6 288.4 %copy-start.3 = (f32[1,1024]{1,0:T(1,128)}, f32[1,1024]{1,0:T(1,128)S(1)}, u32[]{:S(2)}) copy-start(f32[1,1024]{1,0:T(1,128)S(1)} %get-tuple-element.128) | copy-start | bytes 12292
  73.6 288.4 %copy-start.5 = (f32[1,1024]{1,0:T(1,128)}, f32[1,1024]{1,0:T(1,128)S(1)}, u32[]{:S(2)}) copy-start(f32[1,1024]{1,0:T(1,128)S(1)} %get-tuple-element.129) | copy-start | bytes 12292
  73.6 288.4 %copy-start.7 = (f32[1,1024]{1,0:T(1,128)}, f32[1,1024]{1,0:T(1,128)S(1)}, u32[]{:S(2)}) copy-start(f32[1,1024]{1,0:T(1,128)S(1)} %get-tuple-element.130) | copy-start | bytes 12292
  73.6 18.2 %copy-start = (f32[5,4096]{1,0:T(8,128)S(1)}, f32[5,4096]{1,0:T(8,128)}, u32[]{:S(2)}) copy-start(f32[5,4096]{1,0:T(8,128)} %param.21) | copy-start | bytes 245764
  75.3 16.6 %copy-start.1 = (f32[4096]{0:T(1024)S(1)}, f32[4096]{0:T(1024)}, u32[]{:S(2)}) copy-start(f32[4096]{0:T(1024)} %param.23) | copy-start | bytes 49156
  75.3 16.6 %copy-start.9 = (f32[4096]{0:T(1024)S(1)}, f32[4096]{0:T(1024)}, u32[]{:S(2)}) copy-start(f32[4096]{0:T(1024)} %param.24) | copy-start | bytes 49156
  194.6 4.6 collective-permute-start
  201.2 322.6 %reduce-scatter.12.cloned.1.call-start = ((), (), s32[]{:S(2)}) async-start(), calls=%async_computation.5 | async-start | bytes 1179648
  201.3 109.3 %copy-start.13 = (pred[4096]{0:T(1024)(128)(4,1)}, pred[4096]{0:T(1024)(128)(4,1)S(1)}, u32[]{:S(2)}) copy-start(pred[4096]{0:T(1024)(128)(4,1)S(1)} %get-tuple-element.160) | copy-start | bytes 12292
  201.3 109.3 %copy-start.15 = (pred[4096]{0:T(1024)(128)(4,1)}, pred[4096]{0:T(1024)(128)(4,1)S(1)}, u32[]{:S(2)}) copy-start(pred[4096]{0:T(1024)(128)(4,1)S(1)} %get-tuple-element.161) | copy-start | bytes 12292
  201.3 109.3 %copy-start.17 = (pred[4096]{0:T(1024)(128)(4,1)}, pred[4096]{0:T(1024)(128)(4,1)S(1)}, u32[]{:S(2)}) copy-start(pred[4096]{0:T(1024)(128)(4,1)S(1)} %get-tuple-element.162) | copy-start | bytes 12292
  201.3 109.3 %copy-start.19 = (pred[4096]{0:T(1024)(128)(4,1)}, pred[4096]{0:T(1024)(128)(4,1)S(1)}, u32[]{:S(2)}) copy-start(pred[4096]{0:T(1024)(128)(4,1)S(1)} %get-tuple-element.163) | copy-start | bytes 12292
  248.8 5.5 collective-permute-start.1
  319.6 42.4 %copy-start.26 = (f32[1,1024]{1,0:T(1,128)S(1)}, f32[1,1024]{1,0:T(1,128)}, u32[]{:S(2)}) copy-start(f32[1,1024]{1,0:T(1,128)} %get-tuple-element.113) | copy-start | bytes 12292
  319.6 42.4 %copy-start.28 = (f32[1,1024]{1,0:T(1,128)S(1)}, f32[1,1024]{1,0:T(1,128)}, u32[]{:S(2)}) copy-start(f32[1,1024]{1,0:T(1,128)} %get-tuple-element.114) | copy-start | bytes 12292
  319.6 42.4 %copy-start.30 = (f32[1,1024]{1,0:T(1,128)S(1)}, f32[1,1024]{1,0:T(1,128)}, u32[]{:S(2)}) copy-start(f32[1,1024]{1,0:T(1,128)} %get-tuple-element.115) | copy-start | bytes 12292
  319.6 42.4 %copy-start.32 = (f32[1,1024]{1,0:T(1,128)S(1)}, f32[1,1024]{1,0:T(1,128)}, u32[]{:S(2)}) copy-start(f32[1,1024]{1,0:T(1,128)} %get-tuple-element.116) | copy-start | bytes 12292
  481.2 6.3 copy-start.2
  482.3 2.6 collective-permute-start.2
  487.5 409.2 %reduce-scatter.14.cloned.1.call-start = ((), (), s32[]{:S(2)}) async-start(), calls=%async_computation.6 | async-start | bytes 1179648
  487.6 139.4 %copy-start.11 = (f32[4,256]{1,0:T(4,128)}, f32[4,256]{1,0:T(4,128)S(1)}, u32[]{:S(2)}) copy-start(f32[4,256]{1,0:T(4,128)S(1)} %copy.300) | copy-start | bytes 12292
  621.6 5.5 collective-permute-start.3
  693.2 41.3 %copy-start.4 = (f32[1,1024]{1,0:T(1,128)S(1)}, f32[1,1024]{1,0:T(1,128)}, u32[]{:S(2)}) copy-start(f32[1,1024]{1,0:T(1,128)} %copy-done.3) | copy-start | bytes 12292
  693.2 41.3 %copy-start.6 = (f32[1,1024]{1,0:T(1,128)S(1)}, f32[1,1024]{1,0:T(1,128)}, u32[]{:S(2)}) copy-start(f32[1,1024]{1,0:T(1,128)} %copy-done.5) | copy-start | bytes 12292
  693.3 41.3 %copy-start.8 = (f32[1,1024]{1,0:T(1,128)S(1)}, f32[1,1024]{1,0:T(1,128)}, u32[]{:S(2)}) copy-start(f32[1,1024]{1,0:T(1,128)} %copy-done.7) | copy-start | bytes 12292
  693.3 41.4 %copy-start.27 = (f32[1,1024]{1,0:T(1,128)S(1)}, f32[1,1024]{1,0:T(1,128)}, u32[]{:S(2)}) copy-start(f32[1,1024]{1,0:T(1,128)} %get-tuple-element.113) | copy-start | bytes 12292
  693.3 41.4 %copy-start.29 = (f32[1,1024]{1,0:T(1,128)S(1)}, f32[1,1024]{1,0:T(1,128)}, u32[]{:S(2)}) copy-start(f32[1,1024]{1,0:T(1,128)} %get-tuple-element.114) | copy-start | bytes 12292
  693.3 41.4 %copy-start.31 = (f32[1,1024]{1,0:T(1,128)S(1)}, f32[1,1024]{1,0:T(1,128)}, u32[]{:S(2)}) copy-start(f32[1,1024]{1,0:T(1,128)} %get-tuple-element.115) | copy-start | bytes 12292
  693.3 41.4 %copy-start.33 = (f32[1,1024]{1,0:T(1,128)S(1)}, f32[1,1024]{1,0:T(1,128)}, u32[]{:S(2)}) copy-start(f32[1,1024]{1,0:T(1,128)} %get-tuple-element.116) | copy-start | bytes 12292
  734.6 17.5 %copy-start.22 = (pred[4096]{0:T(1024)(128)(4,1)S(1)}, pred[4096]{0:T(1024)(128)(4,1)}, u32[]{:S(2)}) copy-start(pred[4096]{0:T(1024)(128)(4,1)} %copy-done.21) | copy-start | bytes 12292
  853.9 85.1 %copy-start.12 = (f32[4,256]{1,0:T(4,128)S(1)}, f32[4,256]{1,0:T(4,128)}, u32[]{:S(2)}) copy-start(f32[4,256]{1,0:T(4,128)} %copy-done.11) | copy-start | bytes 12292
  855.0 2.8 collective-permute-start.4
  859.7 152.7 %copy-start.14 = (pred[4096]{0:T(1024)(128)(4,1)S(1)}, pred[4096]{0:T(1024)(128)(4,1)}, u32[]{:S(2)}) copy-start(pred[4096]{0:T(1024)(128)(4,1)} %copy-done.13) | copy-start | bytes 12292
  859.8 152.7 %copy-start.16 = (pred[4096]{0:T(1024)(128)(4,1)S(1)}, pred[4096]{0:T(1024)(128)(4,1)}, u32[]{:S(2)}) copy-start(pred[4096]{0:T(1024)(128)(4,1)} %copy-done.15) | copy-start | bytes 12292
  859.8 152.7 %copy-start.18 = (pred[4096]{0:T(1024)(128)(4,1)S(1)}, pred[4096]{0:T(1024)(128)(4,1)}, u32[]{:S(2)}) copy-start(pred[4096]{0:T(1024)(128)(4,1)} %copy-done.17) | copy-start | bytes 12292
  859.8 152.7 %copy-start.20 = (pred[4096]{0:T(1024)(128)(4,1)S(1)}, pred[4096]{0:T(1024)(128)(4,1)}, u32[]{:S(2)}) copy-start(pred[4096]{0:T(1024)(128)(4,1)} %copy-done.19) | copy-start | bytes 12292
  950.3 5.5 collective-permute-start.5
  1012.5 9.0 copy-start.10
Sparse Core Ops, SparseCore 0:
  35.1 37.1 all-reduce.4
  201.3 36.4 reduce-scatter.9
  487.6 36.1 reduce-scatter.11
  859.9 36.7 reduce-scatter.13
